TPU v7x, 256 devices: a whole 4x4x8 slice. The times are simulated.
256 devices in a mesh: gx: 8 (over z), gy: 4 (over y), gz: 8 (over x, core).
Axes of the slice: x: 4, y: 4, z: 8, core: 2. Of those that a mesh axis runs over, the one named last changes fastest.
Arguments:
- schur: bfloat16 [8, 4, 8, 2048, 2048], P('gx', 'gy', 'gz'), may hold values from -0.09375 to 0.09375
- interface_diag: float32 [8, 4, 8, 2048], P('gx', 'gy', 'gz'), may hold values from 2 to 4
- precond: float32 [8, 4, 8, 16, 128, 128], P('gx', 'gy', 'gz'), may hold values from -0.3 to 0.8
- load: bfloat16 [8, 4, 8, 2048, 256], P('gx', 'gy', 'gz'), may hold values from -170 to 170
- face_blocks: int32 [8, 4, 8, 6, 2], P('gx', 'gy', 'gz'), may hold values from 0 to 16, as said below
Outputs:
- solution: float32 [8, 4, 8, 2048, 256], P('gx', 'gy', 'gz')
- residual_norm: float32 [256], replicated
Inputs may be any that keep to these rules, and one draw needn't show every extreme that they name: `face_blocks`: for each subdomain p and direction d (0, 1: next and previous along the first grid dimension; 2, 3 and 4, 5 likewise along the second and third), slots 0 to n - 1 hold block numbers below 16 shared with the neighbour in that direction, where n (1 to 2 inside the grid, 0 across its boundary) equals the neighbour's n for the opposite direction, and the neighbour's slot k of the opposite direction holds the block that shares with p's slot k; the remaining slots hold 16; no block number appears twice in one subdomain's table; some face shares 2 blocks in every draw.
All inputs are finite; a program needn't handle non-finite values.
Results may differ from a plain program's by a relative error of at most 0.0008.
Values sent between devices are 32-bit elements; how exact they have to be, the bound alone decides.
A program may use at most 128 MiB of HBM per device.

v0:
```python
import functools

import jax
import jax.numpy as jnp
from jax import lax
from jax.sharding import Mesh
from jax.sharding import PartitionSpec as P

GZ = ("gz_0", "gz_1")
GX_GY_GZ = ("gx", "gy", "gz_0", "gz_1")


epsilon = 1e-06


def extended_2(value, sides, width):
    for axis, dim in sides:
        peers, length = (lax.axis_size(axis), value.shape[dim])
        up = [(i, (i + 1) % peers) for i in range(peers - 1)]
        down = [(j, i) for i, j in up]
        last = lax.slice_in_dim(value, length - width, length, axis=dim)
        leading = lax.slice_in_dim(value, 0, width, axis=dim)
        before = lax.ppermute(last, axis, up)
        after = lax.ppermute(leading, axis, down)
        value = jnp.concatenate([before, value, after], axis=dim)
    return value


def one_axis_at_a_time(value, axes):
    return functools.reduce(lax.psum, axes, value)


def assemble(blocks, slot_index, live_mask):
    block_count, block_rows, row_width = blocks.shape
    slot_count = slot_index.shape[1]
    extended = jnp.concatenate([blocks, jnp.zeros((1, block_rows, row_width), jnp.float32)], axis=0)
    slot_flat = slot_index.reshape(-1)
    packed = extended[slot_flat].reshape(6, slot_count, block_rows, row_width)
    gx_faces = extended_2(jnp.stack([packed[1], packed[0]], 0), (("gx", 0),), 1)
    gy_faces = extended_2(jnp.stack([packed[3], packed[2]], 0), (("gy", 0),), 1)
    gz_faces = extended_2(jnp.stack([packed[5], packed[4]], 0), ((GZ, 0),), 1)
    arrived = jnp.stack(
        [gx_faces[3], gx_faces[0], gy_faces[3], gy_faces[0], gz_faces[3], gz_faces[0]], 0
    )
    extended = extended.at[slot_flat].add(arrived.reshape(6 * slot_count, block_rows, row_width))
    return extended[:block_count] * live_mask[:, None, None]


def partial_product(left_vec, right_vec):
    return 0.5 * jnp.sum(left_vec * right_vec, axis=(0, 1))


def on_device(schur, interface_diag, precond, load, face_blocks):
    block_count = precond.shape[3]
    block_rows = precond.shape[4]
    rhs_count = load.shape[-1]
    slot_index = face_blocks.reshape(6, face_blocks.shape[-1])
    slot_hits = slot_index[:, :, None] == jnp.arange(block_count, dtype=jnp.int32)
    live_mask = jnp.any(slot_hits, axis=(0, 1)).astype(jnp.float32)
    matrix = schur.reshape(schur.shape[-2], schur.shape[-1])
    diag_column = interface_diag.reshape(-1, 1)
    local_blocks = precond.reshape(block_count, block_rows, block_rows)
    assembled_load = assemble(
        load.reshape(block_count, block_rows, rhs_count).astype(jnp.float32), slot_index, live_mask
    )
    widened = jnp.pad(local_blocks, ((0, 0), (0, 0), (0, rhs_count - block_rows)))
    summed = assemble(widened, slot_index, live_mask)[:, :, :block_rows]

    def precondition(vector):
        return jnp.einsum("bij,bjr->bir", summed, vector, precision=lax.Precision.HIGHEST)

    def operate(vector):
        flattened = vector.reshape(block_count * block_rows, rhs_count)
        narrow = flattened.astype(jnp.bfloat16)
        product = jnp.dot(matrix, narrow, preferred_element_type=jnp.float32)
        partial_value = product + diag_column * flattened
        return assemble(
            partial_value.reshape(block_count, block_rows, rhs_count), slot_index, live_mask
        )

    precond_raw = precondition(assembled_load)
    working_raw = operate(precond_raw)
    load_square, cross_first, raw_square = (
        one_axis_at_a_time(partial_product(assembled_load, assembled_load), GX_GY_GZ),
        one_axis_at_a_time(partial_product(working_raw, assembled_load), GX_GY_GZ),
        one_axis_at_a_time(partial_product(working_raw, working_raw), GX_GY_GZ),
    )
    initial = jnp.sqrt(load_square + epsilon)
    rescale = 1.0 / initial
    basis_first = assembled_load * rescale
    precond_first = precond_raw * rescale
    diag_first = cross_first * rescale * rescale
    working = working_raw * rescale - diag_first * basis_first
    below_first = jnp.sqrt(
        jnp.maximum(raw_square * rescale * rescale - diag_first * diag_first, 0.0) + epsilon
    )
    basis_second = working / below_first
    precond_second = precondition(basis_second)
    working = operate(precond_second)
    upper_second, diag_second, work_square = (
        one_axis_at_a_time(partial_product(working, basis_first), GX_GY_GZ),
        one_axis_at_a_time(partial_product(working, basis_second), GX_GY_GZ),
        one_axis_at_a_time(partial_product(working, working), GX_GY_GZ),
    )
    below_second = jnp.sqrt(
        jnp.maximum(work_square - upper_second * upper_second - diag_second * diag_second, 0.0)
        + epsilon
    )
    radius_first = jnp.sqrt(diag_first * diag_first + below_first * below_first)
    cosine_first = diag_first / radius_first
    sine_first = below_first / radius_first
    rotated_top = cosine_first * upper_second + sine_first * diag_second
    rotated_low = cosine_first * diag_second - sine_first * upper_second
    radius_second = jnp.sqrt(rotated_low * rotated_low + below_second * below_second)
    cosine_second = rotated_low / radius_second
    sine_second = below_second / radius_second
    weight_second = -initial * sine_first * cosine_second / radius_second
    weight_first = (initial * cosine_first - rotated_top * weight_second) / radius_first
    solution = weight_first * precond_first + weight_second * precond_second
    residual_norm = initial * sine_first * sine_second
    return (solution.reshape(1, 1, 1, block_count * block_rows, rhs_count), residual_norm)


def solution(mesh):
    torus = Mesh(
        mesh.devices.reshape(mesh.shape["gx"], mesh.shape["gy"], 4, 2), ("gx", "gy", "gz_0", "gz_1")
    )
    in_specs = (
        P("gx", "gy", GZ, None, None),
        P("gx", "gy", GZ, None),
        P("gx", "gy", GZ, None, None, None),
        P("gx", "gy", GZ, None, None),
        P("gx", "gy", GZ, None, None),
    )
    out_specs = (P("gx", "gy", GZ, None, None), P())
    return jax.shard_map(
        on_device, mesh=torus, in_specs=in_specs, out_specs=out_specs, check_vma=False
    )
```

profile of v0, /device:TPU:1, one launch (start us, length us, event | category | flops | bytes accessed | tf_op | source)
XLA Modules:
  0.0 271.4 jit_solution(16589500102011822868)
XLA Ops:
  13.6 4.5 %collective-permute-start.11 = (f32[1,2,128,256]{3,2,1,0:T(8,128)S(1)}, f32[1,2,128,256]{3,2,1,0:T(8,128)S(1)}, u32[]{:S(2)}, u32[]{:S(2)}) collective-permute-start(f32[1,2,128,256]{3,2,1,0:T(8,128)S(1)} %get-tuple-element.49), channel_id=1, source_target_pairs={{0,1},{1,2},{2,3},{3,4},{4,5},{5,6},{6,7},{8,9},{9,10},{10,11},{11... | collective-permute-start | bytes 786440 | tf_op jit(solution)/shard_map/ppermute | solution.py:23
  20.0 4.9 %collective-permute-start.7 = (f32[1,2,128,256]{3,2,1,0:T(8,128)S(1)}, f32[1,2,128,256]{3,2,1,0:T(8,128)S(1)}, u32[]{:S(2)}, u32[]{:S(2)}) collective-permute-start(f32[1,2,128,256]{3,2,1,0:T(8,128)S(1)} %copy-done.6), channel_id=1, source_target_pairs={{0,32},{32,64},{64,96},{96,128},{128,160},{160,192},{192,224},{1,3... | collective-permute-start | bytes 786440 | tf_op jit(solution)/shard_map/ppermute | solution.py:23
  28.0 4.0 %collective-permute-start.9 = (f32[1,2,128,256]{3,2,1,0:T(8,128)S(1)}, f32[1,2,128,256]{3,2,1,0:T(8,128)S(1)}, u32[]{:S(2)}, u32[]{:S(2)}) collective-permute-start(f32[1,2,128,256]{3,2,1,0:T(8,128)S(1)} %copy-done.4), channel_id=1, source_target_pairs={{0,8},{8,16},{16,24},{1,9},{9,17},{17,25},{2,10},{10,18},{18,26},{... | collective-permute-start | bytes 786440 | tf_op jit(solution)/shard_map/ppermute | solution.py:23
  32.7 4.5 %collective-permute-start.5 = (f32[1,2,128,256]{3,2,1,0:T(8,128)S(1)}, f32[1,2,128,256]{3,2,1,0:T(8,128)}, u32[]{:S(2)}, u32[]{:S(2)}) collective-permute-start(f32[1,2,128,256]{3,2,1,0:T(8,128)S(1)} %get-tuple-element.55), channel_id=1, source_target_pairs={{0,1},{1,2},{2,3},{3,4},{4,5},{5,6},{6,7},{8,9},{9,10},{10,11},{11... | collective-permute-start | bytes 786440 | tf_op jit(solution)/shard_map/ppermute | solution.py:23
  40.6 3.6 %collective-permute-start.1 = (f32[1,2,128,256]{3,2,1,0:T(8,128)S(1)}, f32[1,2,128,256]{3,2,1,0:T(8,128)S(1)}, u32[]{:S(2)}, u32[]{:S(2)}) collective-permute-start(f32[1,2,128,256]{3,2,1,0:T(8,128)S(1)} %get-tuple-element.59), channel_id=1, source_target_pairs={{0,32},{32,64},{64,96},{96,128},{128,160},{160,192},{192,224},{1,3... | collective-permute-start | bytes 786440 | tf_op jit(solution)/shard_map/ppermute | solution.py:23
  47.0 4.0 %collective-permute-start.3 = (f32[1,2,128,256]{3,2,1,0:T(8,128)S(1)}, f32[1,2,128,256]{3,2,1,0:T(8,128)S(1)}, u32[]{:S(2)}, u32[]{:S(2)}) collective-permute-start(f32[1,2,128,256]{3,2,1,0:T(8,128)S(1)} %get-tuple-element.57), channel_id=1, source_target_pairs={{0,8},{8,16},{16,24},{1,9},{9,17},{17,25},{2,10},{10,18},{18,26},{... | collective-permute-start | bytes 786440 | tf_op jit(solution)/shard_map/ppermute | solution.py:23
  54.7 4.5 %scatter_fusion.1 = f32[17,128,256]{2,1,0:T(8,128)} fusion(f32[17,128,256]{2,1,0:T(8,128)} %copy-done, s32[12]{0:T(128)S(1)} %fusion.26, f32[12,128,256]{2,1,0:T(8,128)} %bitcast.17), kind=kCustom, calls=%fused_computation.5 | custom fusion | flops 393216 | bytes 4718640 | tf_op jit(solution)/shard_map/scatter-add | solution.py:45
  66.4 3.1 %scatter_fusion = f32[17,128,256]{2,1,0:T(8,128)S(1)} fusion(f32[17,128,256]{2,1,0:T(8,128)S(1)} %pad_convert_fusion, s32[12]{0:T(128)S(1)} %fusion.26, f32[12,128,256]{2,1,0:T(8,128)} %bitcast.8), kind=kCustom, calls=%fused_computation.4 | custom fusion | flops 393216 | bytes 4718640 | tf_op jit(solution)/shard_map/scatter-add | solution.py:45
  69.5 4.7 %fusion.29 = (bf16[16,128,256]{2,1,0:T(8,128)(2,1)S(1)}, f32[16,128,256]{2,1,0:T(8,128)}) fusion(f32[17,128,256]{2,1,0:T(8,128)S(1)} %scatter_fusion, f32[16]{0:T(128)S(1)} %convert_element_type.26, f32[16,128,256]{2,1,0:T(8,128)} %slice.233), kind=kOutput, calls=%fused_computation.110 | convolution fusion | flops 806617088 | bytes 6292480 | tf_op jit(solution)/shard_map/bij,bjr->bir/dot_general | solution.py:70
  77.1 7.7 %fusion.13 = f32[2048,256]{0,1:T(8,128)} fusion(bf16[2048,256]{1,0:T(8,128)(2,1)S(1)} %bitcast.97, bf16[1,1,1,2048,2048]{4,3,2,1,0:T(8,128)(2,1)} %param.5, f32[2048,256]{0,1:T(8,128)} %copy.20, f32[2048]{0:T(1024)S(1)} %bitcast.99), kind=kOutput, calls=%fused_computation.15 | convolution fusion | flops 2148532224 | bytes 13639680 | tf_op jit(solution)/shard_map/dot_general | solution.py:75
  87.8 3.2 %concatenate.17 = f32[17,128,256]{2,1,0:T(8,128)} pad(f32[16,128,256]{2,1,0:T(8,128)} %bitcast.92, f32[]{:T(128)} %constant.4.clone.1), padding=0_1x0_0x0_0 | pad | bytes 4325380 | tf_op jit(solution)/shard_map/concatenate | solution.py:36
  91.0 3.4 %gather_fusion.2 = f32[12,128,256]{2,1,0:T(8,128)} fusion(f32[17,128,256]{2,1,0:T(8,128)} %concatenate.17, s32[1024]{0:T(1024)S(1)} %pad_clamp_fusion), kind=kCustom, calls=%fused_computation.2 | custom fusion | bytes 3145776 | tf_op jit(solution)/shard_map/gather | solution.py:38
  97.3 4.0 %collective-permute-start.13 = (f32[1,2,128,256]{3,2,1,0:T(8,128)S(1)}, f32[1,2,128,256]{3,2,1,0:T(8,128)S(1)}, u32[]{:S(2)}, u32[]{:S(2)}) collective-permute-start(f32[1,2,128,256]{3,2,1,0:T(8,128)S(1)} %get-tuple-element.47), channel_id=1, source_target_pairs={{0,32},{32,64},{64,96},{96,128},{128,160},{160,192},{192,224},{1,3... | collective-permute-start | bytes 786440 | tf_op jit(solution)/shard_map/ppermute | solution.py:23
  102.6 5.2 %collective-permute-start.17 = (f32[1,2,128,256]{3,2,1,0:T(8,128)S(1)}, f32[1,2,128,256]{3,2,1,0:T(8,128)S(1)}, u32[]{:S(2)}, u32[]{:S(2)}) collective-permute-start(f32[1,2,128,256]{3,2,1,0:T(8,128)S(1)} %get-tuple-element.43), channel_id=1, source_target_pairs={{0,1},{1,2},{2,3},{3,4},{4,5},{5,6},{6,7},{8,9},{9,10},{10,11},{11... | collective-permute-start | bytes 786440 | tf_op jit(solution)/shard_map/ppermute | solution.py:23
  109.7 4.5 %collective-permute-start.15 = (f32[1,2,128,256]{3,2,1,0:T(8,128)S(1)}, f32[1,2,128,256]{3,2,1,0:T(8,128)S(1)}, u32[]{:S(2)}, u32[]{:S(2)}) collective-permute-start(f32[1,2,128,256]{3,2,1,0:T(8,128)S(1)} %get-tuple-element.45), channel_id=1, source_target_pairs={{0,8},{8,16},{16,24},{1,9},{9,17},{17,25},{2,10},{10,18},{18,26},{... | collective-permute-start | bytes 786440 | tf_op jit(solution)/shard_map/ppermute | solution.py:23
  119.6 4.5 %scatter_fusion.2 = f32[17,128,256]{2,1,0:T(8,128)} fusion(f32[17,128,256]{2,1,0:T(8,128)} %concatenate.17, s32[12]{0:T(128)S(1)} %fusion.26, f32[12,128,256]{2,1,0:T(8,128)} %bitcast.30), kind=kCustom, calls=%fused_computation.6 | custom fusion | flops 393216 | bytes 4718640 | tf_op jit(solution)/shard_map/scatter-add | solution.py:45
  126.3 15.5 %all-reduce.6 = (f32[256]{0:T(256)S(1)}, f32[256]{0:T(256)S(1)}, f32[256]{0:T(256)S(1)}) all-reduce(f32[256]{0:T(256)S(1)} %broadcast_multiply_fusion.5, f32[256]{0:T(256)S(1)} %get-tuple-element.66, f32[256]{0:T(256)S(1)} %get-tuple-element.67), channel_id=1, replica_groups=mesh['gx'=8,'gy'=4,'gz_0'=4,'gz_1'=2] {'gx'}, use_global_device_ids=true, to_apply=%region_3.4 | all-reduce | flops 768 | bytes 6144 | tf_op jit(solution)/shard_map/psum | solution.py:30
  141.8 9.5 %all-reduce.10 = (f32[256]{0:T(256)S(1)}, f32[256]{0:T(256)S(1)}, f32[256]{0:T(256)S(1)}) all-reduce(f32[256]{0:T(256)S(1)} %get-tuple-element.11, f32[256]{0:T(256)S(1)} %get-tuple-element.12, f32[256]{0:T(256)S(1)} %get-tuple-element.13), channel_id=1, replica_groups=mesh['gx'=8,'gy'=4,'gz_0'=4,'gz_1'=2] {'gy'}, use_global_device_ids=true, to_apply=%region_4.5 | all-reduce | flops 768 | bytes 6144 | tf_op jit(solution)/shard_map/psum | solution.py:30
  151.3 8.8 %all-reduce.8 = (f32[256]{0:T(256)S(1)}, f32[256]{0:T(256)S(1)}, f32[256]{0:T(256)S(1)}) all-reduce(f32[256]{0:T(256)S(1)} %get-tuple-element.23, f32[256]{0:T(256)S(1)} %get-tuple-element.24, f32[256]{0:T(256)S(1)} %get-tuple-element.25), channel_id=1, replica_groups=mesh['gx'=8,'gy'=4,'gz_0'=4,'gz_1'=2] {'gz_0'}, use_global_device_ids=true, to_apply=%region_5.6 | all-reduce | flops 768 | bytes 6144 | tf_op jit(solution)/shard_map/psum | solution.py:30
  160.1 11.4 %all-reduce.12 = (f32[256]{0:T(256)S(1)}, f32[256]{0:T(256)S(1)}, f32[256]{0:T(256)S(1)}) all-reduce(f32[256]{0:T(256)S(1)} %get-tuple-element.17, f32[256]{0:T(256)S(1)} %get-tuple-element.18, f32[256]{0:T(256)S(1)} %get-tuple-element.19), channel_id=1, replica_groups=mesh['gx'=8,'gy'=4,'gz_0'=4,'gz_1'=2] {'gz_1'}, use_global_device_ids=true, to_apply=%region_6.7 | all-reduce | flops 768 | bytes 6144 | tf_op jit(solution)/shard_map/psum | solution.py:30
  174.1 3.3 %fusion.30 = (bf16[16,128,256]{2,1,0:T(8,128)(2,1)S(1)}, f32[16,128,256]{2,1,0:T(8,128)}) fusion(f32[16,128,256]{2,1,0:T(8,128)S(1)} %subtract_divide_fusion, f32[16,128,256]{2,1,0:T(8,128)S(1)} %copy-done.2, f32[16]{0:T(128)S(1)} %convert_element_type.26), kind=kOutput, calls=%fused_computation.111 | convolution fusion | flops 806092800 | bytes 6291968 | tf_op jit(solution)/shard_map/bij,bjr->bir/dot_general | solution.py:70
  180.3 7.7 %fusion.10 = f32[2048,256]{0,1:T(8,128)} fusion(bf16[2048,256]{1,0:T(8,128)(2,1)S(1)} %bitcast.95, bf16[1,1,1,2048,2048]{4,3,2,1,0:T(8,128)(2,1)} %param.5, f32[2048,256]{0,1:T(8,128)} %copy.24, f32[2048]{0:T(1024)S(1)} %bitcast.100), kind=kOutput, calls=%fused_computation.14 | convolution fusion | flops 2148532224 | bytes 13639680 | tf_op jit(solution)/shard_map/dot_general | solution.py:75
  190.9 3.2 %concatenate.18 = f32[17,128,256]{2,1,0:T(8,128)} pad(f32[16,128,256]{2,1,0:T(8,128)} %bitcast.91, f32[]{:T(128)} %constant.4.clone.1), padding=0_1x0_0x0_0 | pad | bytes 4325380 | tf_op jit(solution)/shard_map/concatenate | solution.py:36
  194.2 3.4 %gather_fusion.3 = f32[12,128,256]{2,1,0:T(8,128)} fusion(f32[17,128,256]{2,1,0:T(8,128)} %concatenate.18, s32[1024]{0:T(1024)S(1)} %pad_clamp_fusion), kind=kCustom, calls=%fused_computation.3 | custom fusion | bytes 3145776 | tf_op jit(solution)/shard_map/gather | solution.py:38
  200.4 4.0 %collective-permute-start.19 = (f32[1,2,128,256]{3,2,1,0:T(8,128)S(1)}, f32[1,2,128,256]{3,2,1,0:T(8,128)S(1)}, u32[]{:S(2)}, u32[]{:S(2)}) collective-permute-start(f32[1,2,128,256]{3,2,1,0:T(8,128)S(1)} %get-tuple-element.41), channel_id=1, source_target_pairs={{0,32},{32,64},{64,96},{96,128},{128,160},{160,192},{192,224},{1,3... | collective-permute-start | bytes 786440 | tf_op jit(solution)/shard_map/ppermute | solution.py:23
  210.5 4.3 %collective-permute-start.21 = (f32[1,2,128,256]{3,2,1,0:T(8,128)S(1)}, f32[1,2,128,256]{3,2,1,0:T(8,128)S(1)}, u32[]{:S(2)}, u32[]{:S(2)}) collective-permute-start(f32[1,2,128,256]{3,2,1,0:T(8,128)S(1)} %get-tuple-element.39), channel_id=1, source_target_pairs={{0,8},{8,16},{16,24},{1,9},{9,17},{17,25},{2,10},{10,18},{18,26},{... | collective-permute-start | bytes 786440 | tf_op jit(solution)/shard_map/ppermute | solution.py:23
  222.2 4.5 %scatter_fusion.3 = f32[17,128,256]{2,1,0:T(8,128)} fusion(f32[17,128,256]{2,1,0:T(8,128)} %concatenate.18, s32[12]{0:T(128)S(1)} %fusion.26, f32[12,128,256]{2,1,0:T(8,128)} %bitcast.41), kind=kCustom, calls=%fused_computation.7 | custom fusion | flops 393216 | bytes 4718640 | tf_op jit(solution)/shard_map/scatter-add | solution.py:45
  229.6 12.0 %all-reduce.5 = (f32[256]{0:T(256)S(1)}, f32[256]{0:T(256)S(1)}, f32[256]{0:T(256)S(1)}) all-reduce(f32[256]{0:T(256)S(1)} %broadcast_multiply_fusion.1, f32[256]{0:T(256)S(1)} %broadcast_multiply_fusion, f32[256]{0:T(256)S(1)} %broadcast_multiply_fusion.2), channel_id=1, replica_groups=mesh['gx'=8,'gy'=4,'gz_0'=4,'gz_1'=2] {'gx'}, use_global_device_ids=true, to_apply=%region_26.27 | all-reduce | flops 768 | bytes 6144 | tf_op jit(solution)/shard_map/psum | solution.py:30
  241.6 8.1 %all-reduce.9 = (f32[256]{0:T(256)S(1)}, f32[256]{0:T(256)S(1)}, f32[256]{0:T(256)S(1)}) all-reduce(f32[256]{0:T(256)S(1)} %get-tuple-element.8, f32[256]{0:T(256)S(1)} %get-tuple-element.9, f32[256]{0:T(256)S(1)} %get-tuple-element.10), channel_id=1, replica_groups=mesh['gx'=8,'gy'=4,'gz_0'=4,'gz_1'=2] {'gy'}, use_global_device_ids=true, to_apply=%region_27.28 | all-reduce | flops 768 | bytes 6144 | tf_op jit(solution)/shard_map/psum | solution.py:30
  249.7 6.0 %all-reduce.7 = (f32[256]{0:T(256)S(1)}, f32[256]{0:T(256)S(1)}, f32[256]{0:T(256)S(1)}) all-reduce(f32[256]{0:T(256)S(1)} %get-tuple-element.20, f32[256]{0:T(256)S(1)} %get-tuple-element.21, f32[256]{0:T(256)S(1)} %get-tuple-element.22), channel_id=1, replica_groups=mesh['gx'=8,'gy'=4,'gz_0'=4,'gz_1'=2] {'gz_0'}, use_global_device_ids=true, to_apply=%region_28.29 | all-reduce | flops 768 | bytes 6144 | tf_op jit(solution)/shard_map/psum | solution.py:30
  255.7 11.2 %all-reduce.11 = (f32[256]{0:T(256)S(1)}, f32[256]{0:T(256)S(1)}, f32[256]{0:T(256)S(1)}) all-reduce(f32[256]{0:T(256)S(1)} %get-tuple-element.14, f32[256]{0:T(256)S(1)} %get-tuple-element.15, f32[256]{0:T(256)S(1)} %get-tuple-element.16), channel_id=1, replica_groups=mesh['gx'=8,'gy'=4,'gz_0'=4,'gz_1'=2] {'gz_1'}, use_global_device_ids=true, to_apply=%region_29.30 | all-reduce | flops 768 | bytes 6144 | tf_op jit(solution)/shard_map/psum | solution.py:30
  267.5 3.9 %multiply_add_fusion = f32[16,128,256]{2,1,0:T(8,128)} fusion(f32[16,128,256]{2,1,0:T(8,128)} %get-tuple-element.65, f32[16,128,256]{2,1,0:T(8,128)} %get-tuple-element.63, f32[256]{0:T(256)S(1)} %get-tuple-element.33, f32[256]{0:T(256)S(1)} %get-tuple-element.32, f32[256]{0:T(256)S(1)} %get-tuple-element.36), kind=kLoop, calls=%fused_computation.19 | loop fusion | flops 2097152 | bytes 6294528 | tf_op jit(solution)/shard_map/add | solution.py:119
  (108 shorter events, 83.2 us)
Async XLA Ops:
  3.0 4.4 %copy-start = (f32[17,128,256]{2,1,0:T(8,128)}, f32[17,128,256]{2,1,0:T(8,128)S(1)}, u32[]{:S(2)}) copy-start(f32[17,128,256]{2,1,0:T(8,128)S(1)} %pad.14) | copy-start | bytes 6684676
  4.8 3.8 %copy-start.3 = (bf16[1,1,1,2048,256]{4,3,2,1,0:T(8,128)(2,1)S(1)}, bf16[1,1,1,2048,256]{4,3,2,1,0:T(8,128)(2,1)}, u32[]{:S(2)}) copy-start(bf16[1,1,1,2048,256]{4,3,2,1,0:T(8,128)(2,1)} %param.8) | copy-start | bytes 3145732
  7.3 17.7 %collective-permute-start.6 = (f32[1,2,128,256]{3,2,1,0:T(8,128)}, f32[1,2,128,256]{3,2,1,0:T(8,128)}, u32[]{:S(2)}, u32[]{:S(2)}) collective-permute-start(f32[1,2,128,256]{3,2,1,0:T(8,128)} %get-tuple-element.54), channel_id=1, source_target_pairs={{32,0},{64,32},{96,64},{128,96},{160,128},{192,160},{224,192},{33,... | collective-permute-start | bytes 786440 | tf_op jit(solution)/shard_map/ppermute | solution.py:24
  10.7 9.3 %copy-start.6 = (f32[1,2,128,256]{3,2,1,0:T(8,128)S(1)}, f32[1,2,128,256]{3,2,1,0:T(8,128)}, u32[]{:S(2)}) copy-start(f32[1,2,128,256]{3,2,1,0:T(8,128)} %get-tuple-element.53) | copy-start | bytes 786436
  10.7 14.3 %copy-start.7 = (s32[1,1,1,6,2]{3,4,2,1,0:T(2,128)S(1)}, s32[1,1,1,6,2]{3,4,2,1,0:T(2,128)}, u32[]{:S(2)}) copy-start(s32[1,1,1,6,2]{3,4,2,1,0:T(2,128)} %param.9) | copy-start | bytes 148
  10.7 14.4 %copy-start.5 = (f32[1,2,128,256]{3,2,1,0:T(8,128)S(1)}, f32[1,2,128,256]{3,2,1,0:T(8,128)}, u32[]{:S(2)}) copy-start(f32[1,2,128,256]{3,2,1,0:T(8,128)} %get-tuple-element.52) | copy-start | bytes 786436
  10.7 17.4 %copy-start.4 = (f32[1,2,128,256]{3,2,1,0:T(8,128)S(1)}, f32[1,2,128,256]{3,2,1,0:T(8,128)}, u32[]{:S(2)}) copy-start(f32[1,2,128,256]{3,2,1,0:T(8,128)} %get-tuple-element.51) | copy-start | bytes 786436
  12.3 15.8 %collective-permute-start = (f32[1,2,128,256]{3,2,1,0:T(8,128)S(1)}, f32[1,2,128,256]{3,2,1,0:T(8,128)S(1)}, u32[]{:S(2)}, u32[]{:S(2)}) collective-permute-start(f32[1,2,128,256]{3,2,1,0:T(8,128)S(1)} %get-tuple-element.60), channel_id=1, source_target_pairs={{32,0},{64,32},{96,64},{128,96},{160,128},{192,160},{224,192},{33,... | collective-permute-start | bytes 786440 | tf_op jit(solution)/shard_map/ppermute | solution.py:24
  13.6 33.4 %collective-permute-start.11 = (f32[1,2,128,256]{3,2,1,0:T(8,128)S(1)}, f32[1,2,128,256]{3,2,1,0:T(8,128)S(1)}, u32[]{:S(2)}, u32[]{:S(2)}) collective-permute-start(f32[1,2,128,256]{3,2,1,0:T(8,128)S(1)} %get-tuple-element.49), channel_id=1, source_target_pairs={{0,1},{1,2},{2,3},{3,4},{4,5},{5,6},{6,7},{8,9},{9,10},{10,11},{11... | collective-permute-start | bytes 786440 | tf_op jit(solution)/shard_map/ppermute | solution.py:23
  18.1 26.9 %collective-permute-start.10 = (f32[1,2,128,256]{3,2,1,0:T(8,128)S(1)}, f32[1,2,128,256]{3,2,1,0:T(8,128)S(1)}, u32[]{:S(2)}, u32[]{:S(2)}) collective-permute-start(f32[1,2,128,256]{3,2,1,0:T(8,128)S(1)} %get-tuple-element.50), channel_id=1, source_target_pairs={{1,0},{2,1},{3,2},{4,3},{5,4},{6,5},{7,6},{9,8},{10,9},{11,10},{12... | collective-permute-start | bytes 786440 | tf_op jit(solution)/shard_map/ppermute | solution.py:24
  20.0 12.7 %collective-permute-start.7 = (f32[1,2,128,256]{3,2,1,0:T(8,128)S(1)}, f32[1,2,128,256]{3,2,1,0:T(8,128)S(1)}, u32[]{:S(2)}, u32[]{:S(2)}) collective-permute-start(f32[1,2,128,256]{3,2,1,0:T(8,128)S(1)} %copy-done.6), channel_id=1, source_target_pairs={{0,32},{32,64},{64,96},{96,128},{128,160},{160,192},{192,224},{1,3... | collective-permute-start | bytes 786440 | tf_op jit(solution)/shard_map/ppermute | solution.py:23
  25.1 12.9 %collective-permute-start.8 = (f32[1,2,128,256]{3,2,1,0:T(8,128)S(1)}, f32[1,2,128,256]{3,2,1,0:T(8,128)S(1)}, u32[]{:S(2)}, u32[]{:S(2)}) collective-permute-start(f32[1,2,128,256]{3,2,1,0:T(8,128)S(1)} %copy-done.5), channel_id=1, source_target_pairs={{8,0},{16,8},{24,16},{9,1},{17,9},{25,17},{10,2},{18,10},{26,18},{... | collective-permute-start | bytes 786440 | tf_op jit(solution)/shard_map/ppermute | solution.py:24
  28.0 12.6 %collective-permute-start.9 = (f32[1,2,128,256]{3,2,1,0:T(8,128)S(1)}, f32[1,2,128,256]{3,2,1,0:T(8,128)S(1)}, u32[]{:S(2)}, u32[]{:S(2)}) collective-permute-start(f32[1,2,128,256]{3,2,1,0:T(8,128)S(1)} %copy-done.4), channel_id=1, source_target_pairs={{0,8},{8,16},{16,24},{1,9},{9,17},{17,25},{2,10},{10,18},{18,26},{... | collective-permute-start | bytes 786440 | tf_op jit(solution)/shard_map/ppermute | solution.py:23
  32.7 32.0 %collective-permute-start.5 = (f32[1,2,128,256]{3,2,1,0:T(8,128)S(1)}, f32[1,2,128,256]{3,2,1,0:T(8,128)}, u32[]{:S(2)}, u32[]{:S(2)}) collective-permute-start(f32[1,2,128,256]{3,2,1,0:T(8,128)S(1)} %get-tuple-element.55), channel_id=1, source_target_pairs={{0,1},{1,2},{2,3},{3,4},{4,5},{5,6},{6,7},{8,9},{9,10},{10,11},{11... | collective-permute-start | bytes 786440 | tf_op jit(solution)/shard_map/ppermute | solution.py:23
  38.0 25.1 %collective-permute-start.4 = (f32[1,2,128,256]{3,2,1,0:T(8,128)S(1)}, f32[1,2,128,256]{3,2,1,0:T(8,128)}, u32[]{:S(2)}, u32[]{:S(2)}) collective-permute-start(f32[1,2,128,256]{3,2,1,0:T(8,128)S(1)} %get-tuple-element.56), channel_id=1, source_target_pairs={{1,0},{2,1},{3,2},{4,3},{5,4},{6,5},{7,6},{9,8},{10,9},{11,10},{12... | collective-permute-start | bytes 786440 | tf_op jit(solution)/shard_map/ppermute | solution.py:24
  40.6 11.1 %collective-permute-start.1 = (f32[1,2,128,256]{3,2,1,0:T(8,128)S(1)}, f32[1,2,128,256]{3,2,1,0:T(8,128)S(1)}, u32[]{:S(2)}, u32[]{:S(2)}) collective-permute-start(f32[1,2,128,256]{3,2,1,0:T(8,128)S(1)} %get-tuple-element.59), channel_id=1, source_target_pairs={{0,32},{32,64},{64,96},{96,128},{128,160},{160,192},{192,224},{1,3... | collective-permute-start | bytes 786440 | tf_op jit(solution)/shard_map/ppermute | solution.py:23
  45.0 9.0 %collective-permute-start.2 = (f32[1,2,128,256]{3,2,1,0:T(8,128)S(1)}, f32[1,2,128,256]{3,2,1,0:T(8,128)S(1)}, u32[]{:S(2)}, u32[]{:S(2)}) collective-permute-start(f32[1,2,128,256]{3,2,1,0:T(8,128)S(1)} %get-tuple-element.58), channel_id=1, source_target_pairs={{8,0},{16,8},{24,16},{9,1},{17,9},{25,17},{10,2},{18,10},{26,18},{... | collective-permute-start | bytes 786440 | tf_op jit(solution)/shard_map/ppermute | solution.py:24
  47.0 15.4 %collective-permute-start.3 = (f32[1,2,128,256]{3,2,1,0:T(8,128)S(1)}, f32[1,2,128,256]{3,2,1,0:T(8,128)S(1)}, u32[]{:S(2)}, u32[]{:S(2)}) collective-permute-start(f32[1,2,128,256]{3,2,1,0:T(8,128)S(1)} %get-tuple-element.57), channel_id=1, source_target_pairs={{0,8},{8,16},{16,24},{1,9},{9,17},{17,25},{2,10},{10,18},{18,26},{... | collective-permute-start | bytes 786440 | tf_op jit(solution)/shard_map/ppermute | solution.py:23
  74.2 3.0 %copy-start.8 = (f32[1,1,1,2048]{3,2,1,0:T(1,128)S(1)}, f32[1,1,1,2048]{3,2,1,0:T(1,128)}, u32[]{:S(2)}) copy-start(f32[1,1,1,2048]{3,2,1,0:T(1,128)} %param.6) | copy-start | bytes 24580
  96.0 13.7 %collective-permute-start.12 = (f32[1,2,128,256]{3,2,1,0:T(8,128)S(1)}, f32[1,2,128,256]{3,2,1,0:T(8,128)S(1)}, u32[]{:S(2)}, u32[]{:S(2)}) collective-permute-start(f32[1,2,128,256]{3,2,1,0:T(8,128)S(1)} %get-tuple-element.48), channel_id=1, source_target_pairs={{32,0},{64,32},{96,64},{128,96},{160,128},{192,160},{224,192},{33,... | collective-permute-start | bytes 786440 | tf_op jit(solution)/shard_map/ppermute | solution.py:24
  97.3 17.6 %collective-permute-start.13 = (f32[1,2,128,256]{3,2,1,0:T(8,128)S(1)}, f32[1,2,128,256]{3,2,1,0:T(8,128)S(1)}, u32[]{:S(2)}, u32[]{:S(2)}) collective-permute-start(f32[1,2,128,256]{3,2,1,0:T(8,128)S(1)} %get-tuple-element.47), channel_id=1, source_target_pairs={{0,32},{32,64},{64,96},{96,128},{128,160},{160,192},{192,224},{1,3... | collective-permute-start | bytes 786440 | tf_op jit(solution)/shard_map/ppermute | solution.py:23
  101.3 14.3 %collective-permute-start.14 = (f32[1,2,128,256]{3,2,1,0:T(8,128)S(1)}, f32[1,2,128,256]{3,2,1,0:T(8,128)S(1)}, u32[]{:S(2)}, u32[]{:S(2)}) collective-permute-start(f32[1,2,128,256]{3,2,1,0:T(8,128)S(1)} %get-tuple-element.46), channel_id=1, source_target_pairs={{8,0},{16,8},{24,16},{9,1},{17,9},{25,17},{10,2},{18,10},{26,18},{... | collective-permute-start | bytes 786440 | tf_op jit(solution)/shard_map/ppermute | solution.py:24
  102.6 16.3 %collective-permute-start.17 = (f32[1,2,128,256]{3,2,1,0:T(8,128)S(1)}, f32[1,2,128,256]{3,2,1,0:T(8,128)S(1)}, u32[]{:S(2)}, u32[]{:S(2)}) collective-permute-start(f32[1,2,128,256]{3,2,1,0:T(8,128)S(1)} %get-tuple-element.43), channel_id=1, source_target_pairs={{0,1},{1,2},{2,3},{3,4},{4,5},{5,6},{6,7},{8,9},{9,10},{10,11},{11... | collective-permute-start | bytes 786440 | tf_op jit(solution)/shard_map/ppermute | solution.py:23
  107.8 10.4 %collective-permute-start.16 = (f32[1,2,128,256]{3,2,1,0:T(8,128)S(1)}, f32[1,2,128,256]{3,2,1,0:T(8,128)S(1)}, u32[]{:S(2)}, u32[]{:S(2)}) collective-permute-start(f32[1,2,128,256]{3,2,1,0:T(8,128)S(1)} %get-tuple-element.44), channel_id=1, source_target_pairs={{1,0},{2,1},{3,2},{4,3},{5,4},{6,5},{7,6},{9,8},{10,9},{11,10},{12... | collective-permute-start | bytes 786440 | tf_op jit(solution)/shard_map/ppermute | solution.py:24
  109.7 7.7 %collective-permute-start.15 = (f32[1,2,128,256]{3,2,1,0:T(8,128)S(1)}, f32[1,2,128,256]{3,2,1,0:T(8,128)S(1)}, u32[]{:S(2)}, u32[]{:S(2)}) collective-permute-start(f32[1,2,128,256]{3,2,1,0:T(8,128)S(1)} %get-tuple-element.45), channel_id=1, source_target_pairs={{0,8},{8,16},{16,24},{1,9},{9,17},{17,25},{2,10},{10,18},{18,26},{... | collective-permute-start | bytes 786440 | tf_op jit(solution)/shard_map/ppermute | solution.py:23
  174.0 3.3 %copy-start.1 = (f32[16,128,256]{2,1,0:T(8,128)}, f32[16,128,256]{2,1,0:T(8,128)S(1)}, u32[]{:S(2)}) copy-start(f32[16,128,256]{2,1,0:T(8,128)S(1)} %subtract_divide_fusion) | copy-start | bytes 6291460
  199.1 11.4 %collective-permute-start.18 = (f32[1,2,128,256]{3,2,1,0:T(8,128)S(1)}, f32[1,2,128,256]{3,2,1,0:T(8,128)S(1)}, u32[]{:S(2)}, u32[]{:S(2)}) collective-permute-start(f32[1,2,128,256]{3,2,1,0:T(8,128)S(1)} %get-tuple-element.42), channel_id=1, source_target_pairs={{32,0},{64,32},{96,64},{128,96},{160,128},{192,160},{224,192},{33,... | collective-permute-start | bytes 786440 | tf_op jit(solution)/shard_map/ppermute | solution.py:24
  200.4 15.1 %collective-permute-start.19 = (f32[1,2,128,256]{3,2,1,0:T(8,128)S(1)}, f32[1,2,128,256]{3,2,1,0:T(8,128)S(1)}, u32[]{:S(2)}, u32[]{:S(2)}) collective-permute-start(f32[1,2,128,256]{3,2,1,0:T(8,128)S(1)} %get-tuple-element.41), channel_id=1, source_target_pairs={{0,32},{32,64},{64,96},{96,128},{128,160},{160,192},{192,224},{1,3... | collective-permute-start | bytes 786440 | tf_op jit(solution)/shard_map/ppermute | solution.py:23
  204.4 11.9 %collective-permute-start.20 = (f32[1,2,128,256]{3,2,1,0:T(8,128)S(1)}, f32[1,2,128,256]{3,2,1,0:T(8,128)S(1)}, u32[]{:S(2)}, u32[]{:S(2)}) collective-permute-start(f32[1,2,128,256]{3,2,1,0:T(8,128)S(1)} %get-tuple-element.40), channel_id=1, source_target_pairs={{8,0},{16,8},{24,16},{9,1},{17,9},{25,17},{10,2},{18,10},{26,18},{... | collective-permute-start | bytes 786440 | tf_op jit(solution)/shard_map/ppermute | solution.py:24
  205.7 15.8 %collective-permute-start.23 = (f32[1,2,128,256]{3,2,1,0:T(8,128)S(1)}, f32[1,2,128,256]{3,2,1,0:T(8,128)S(1)}, u32[]{:S(2)}, u32[]{:S(2)}) collective-permute-start(f32[1,2,128,256]{3,2,1,0:T(8,128)S(1)} %get-tuple-element.37), channel_id=1, source_target_pairs={{0,1},{1,2},{2,3},{3,4},{4,5},{5,6},{6,7},{8,9},{9,10},{10,11},{11... | collective-permute-start | bytes 786440 | tf_op jit(solution)/shard_map/ppermute | solution.py:23
  208.6 12.2 %collective-permute-start.22 = (f32[1,2,128,256]{3,2,1,0:T(8,128)S(1)}, f32[1,2,128,256]{3,2,1,0:T(8,128)S(1)}, u32[]{:S(2)}, u32[]{:S(2)}) collective-permute-start(f32[1,2,128,256]{3,2,1,0:T(8,128)S(1)} %get-tuple-element.38), channel_id=1, source_target_pairs={{1,0},{2,1},{3,2},{4,3},{5,4},{6,5},{7,6},{9,8},{10,9},{11,10},{12... | collective-permute-start | bytes 786440 | tf_op jit(solution)/shard_map/ppermute | solution.py:24
  210.5 9.5 %collective-permute-start.21 = (f32[1,2,128,256]{3,2,1,0:T(8,128)S(1)}, f32[1,2,128,256]{3,2,1,0:T(8,128)S(1)}, u32[]{:S(2)}, u32[]{:S(2)}) collective-permute-start(f32[1,2,128,256]{3,2,1,0:T(8,128)S(1)} %get-tuple-element.39), channel_id=1, source_target_pairs={{0,8},{8,16},{16,24},{1,9},{9,17},{17,25},{2,10},{10,18},{18,26},{... | collective-permute-start | bytes 786440 | tf_op jit(solution)/shard_map/ppermute | solution.py:23
  (1 other events, 2.4 us)
where the time goes:
time: 273 us; the launch traced here: 271 us
  blocking collectives  82.6 us (30%)
  starting transfers between devices  68.3 us (25%)
  local copies, waits for them, and re-layouts  61.4 us (22%)
  other arithmetic  28.9 us (11%)
  matrix products  23.4 us (9%)
  waiting for transfers between devices  5.76 us (2%)
    psum x8, blocking collectives, one_axis_at_a_time(): return functools.reduce(lax.psum, axes, value)  82.6 us
    ppermute x12, starting transfers between devices, extended_2(): before = lax.ppermute(last, axis, up)  50.3 us
    ppermute x12, starting transfers between devices, extended_2(): after = lax.ppermute(leading, axis, down)  18 us
    unnamed x39, local copies, waits for them, and re-layouts  17.2 us
    scatter-add x4, other arithmetic, assemble(): extended.at[slot_flat]  16.5 us
    dot_general x2, matrix products, operate(): product = jnp.dot(matrix, narrow, preferred_element_type=jnp.float32)  15.4 us
    gather x4, local copies, waits for them, and re-layouts, assemble(): packed = extended[slot_flat].reshape(6, slot_count, block_rows, row_width)  10.5 us
    dot_general x2, matrix products, precondition(): jnp.einsum('bij,bjr->bir', summed, vector, precision=lax.Precision.HIGHEST)  7.94 us
  transfers between devices with their start and end apart: 24, of which 3 were waited for; matrix products, arithmetic and copies ran while one was open for 10% of the time, Pallas kernels for 0%

commit v1 on v0

v1 whole, which is shorter than its diff:
```python
import jax
import jax.numpy as jnp
from jax import lax
from jax.experimental import pallas as pl
from jax.experimental.pallas import tpu as pltpu
from jax.sharding import PartitionSpec as P

EPS = 1e-06
B = 128
NB = 16
NS = 12
W = 128
H = 2
N = NB * B
C = NS * B
AXES = ("gx", "gy", "gz")
MESH = pl.DeviceIdType.MESH

L0, PM, L1, U10, U11, U20, U21 = range(7)


def fold(x):
    n = x.shape[0]
    while n > 8:
        n //= 2
        x = x[:n] + x[n:]
    return x


def colsum(x):
    return jnp.sum(x, axis=0, keepdims=True)


def split(x):
    hi = x.astype(jnp.bfloat16)
    lo = (x - hi.astype(jnp.float32)).astype(jnp.bfloat16)
    return hi, lo


def main_kernel(sizes, face, s_hbm, d_hbm, p_hbm, l_hbm, out, norm,
                z1, z2, sv, lb, pv, dv, sc, dcol, send_l, recv_l, r, send_p, recv_p, mhl, zb,
                u1, ru1, w1, u2, ru2, red_a, red_b, local_sem, send_sem, recv_sem,
                red_send, red_recv):
    pos = [lax.axis_index(a) for a in AXES]

    def peer(axis, index):
        ids = list(pos)
        ids[axis] = index
        return tuple(ids)

    barrier = pltpu.get_barrier_semaphore()
    peers = 0
    for axis in range(3):
        for off in range(1, sizes[axis]):
            other = lax.rem(pos[axis] + off, sizes[axis])
            pl.semaphore_signal(barrier, inc=1, device_id=peer(axis, other), device_id_type=MESH)
            peers += 1

    loads = [
        pltpu.make_async_copy(l_hbm, lb, local_sem.at[0]),
        pltpu.make_async_copy(p_hbm, pv, local_sem.at[1]),
        pltpu.make_async_copy(d_hbm, dv, local_sem.at[2]),
    ]
    loads += [
        pltpu.make_async_copy(s_hbm.at[:, :, pl.ds(t * B, B)], sv.at[t], local_sem.at[3 + t])
        for t in range(NB)
    ]
    for copy in loads:
        copy.start()

    def exists(d):
        axis = d // 2
        if d % 2 == 0:
            return pos[axis] < sizes[axis] - 1
        return pos[axis] > 0

    def slot(s):
        number = face[0, 0, 0, s // 2, s % 2]
        valid = number < NB
        return jnp.minimum(number, NB - 1), valid

    def message(m, d):
        axis = d // 2
        opp = d + 1 if d % 2 == 0 else d - 1
        step = 1 if d % 2 == 0 else sizes[axis] - 1
        other = lax.rem(pos[axis] + step, sizes[axis])
        if m in (L0, L1):
            h = 0 if m == L0 else 1
            src, dst = send_l.at[h, pl.ds(2 * d, 2)], recv_l.at[h, pl.ds(2 * opp, 2)]
        elif m == PM:
            src, dst = send_p.at[pl.ds(2 * d, 2)], recv_p.at[pl.ds(2 * opp, 2)]
        elif m in (U10, U11):
            h = m - U10
            src, dst = u1.at[h, pl.ds(2 * d, 2)], ru1.at[h, pl.ds(2 * opp, 2)]
        else:
            h = m - U20
            src, dst = u2.at[h, 2 * d + d % 2], ru2.at[h, opp]
        return pltpu.make_async_remote_copy(
            src_ref=src, dst_ref=dst, send_sem=send_sem.at[m, d], recv_sem=recv_sem.at[m, opp],
            device_id=peer(axis, other), device_id_type=MESH)

    def arrival(m, d):
        axis = d // 2
        step = 1 if d % 2 == 0 else sizes[axis] - 1
        other = lax.rem(pos[axis] + step, sizes[axis])
        if m in (L0, L1):
            h = 0 if m == L0 else 1
            src, dst = send_l.at[h, pl.ds(2 * d, 2)], recv_l.at[h, pl.ds(2 * d, 2)]
        elif m == PM:
            src, dst = send_p.at[pl.ds(2 * d, 2)], recv_p.at[pl.ds(2 * d, 2)]
        elif m in (U10, U11):
            h = m - U10
            src, dst = u1.at[h, pl.ds(2 * d, 2)], ru1.at[h, pl.ds(2 * d, 2)]
        else:
            h = m - U20
            src, dst = u2.at[h, 2 * d + d % 2], ru2.at[h, d]
        return pltpu.make_async_remote_copy(
            src_ref=src, dst_ref=dst, send_sem=send_sem.at[m, d], recv_sem=recv_sem.at[m, d],
            device_id=peer(axis, other), device_id_type=MESH)

    def send(m, d):
        @pl.when(exists(d))
        def _():
            message(m, d).start()

    def receive(m, d):
        @pl.when(exists(d))
        def _():
            arrival(m, d).wait_recv()

    loads[0].wait()
    for s in range(NS):
        block, valid = slot(s)
        mask = jnp.where(valid, 1.0, 0.0)
        rows = lb[block].astype(jnp.float32) * mask
        for h in range(H):
            send_l[h, s] = rows[:, h * W:(h + 1) * W]
    loads[1].wait()
    for s in range(NS):
        block, valid = slot(s)
        send_p[s] = pv[block] * jnp.where(valid, 1.0, 0.0)

    pl.semaphore_wait(barrier, peers)
    for m in (L0, PM, L1):
        for d in range(6):
            send(m, d)

    for d in range(6):
        @pl.when(jnp.logical_not(exists(d)))
        def _():
            zero = jnp.zeros((2, B, W), jnp.float32)
            for h in range(H):
                recv_l[h, pl.ds(2 * d, 2)] = zero
                ru1[h, pl.ds(2 * d, 2)] = zero
                ru2[h, d] = zero[0]
            recv_p[pl.ds(2 * d, 2)] = zero

    loads[2].wait()
    for s in range(NS):
        block, valid = slot(s)
        row = dv[block] * jnp.where(valid, 1.0, 0.0)
        dcol[s] = jnp.transpose(jnp.broadcast_to(row, (B, B)))

    for copy in loads[3:]:
        copy.wait()

    @pl.loop(0, 6)
    def _(d):
        for k in range(2):
            number = face[0, 0, 0, d, k]
            mask = jnp.where(number < NB, 1.0, 0.0).astype(jnp.bfloat16)
            top = jnp.minimum(number, NB - 1)
            for t in range(NS):
                block, _ = slot(t)
                sc[pl.ds(pl.multiple_of((2 * d + k) * B, B), B), t * B:(t + 1) * B] = (
                    sv[block, top] * mask)

    def apply_m(s, x):
        hi, lo = split(x)
        both = jnp.concatenate([hi, lo], axis=1)
        rhs = jnp.concatenate([both, both], axis=0)
        out = jnp.dot(mhl[s], rhs, preferred_element_type=jnp.float32)
        return out[:, :W] + out[:, W:]

    def product(h, d, z, u):
        rows = jnp.dot(sc[2 * d * B:2 * (d + 1) * B, :], zb[h], preferred_element_type=jnp.float32)
        for k in range(2):
            s = 2 * d + k
            u[h, s] = rows[k * B:(k + 1) * B] + dcol[s] * z[h, s]

    def red_copy(buf, which, axis, off, target):
        n = sizes[axis]
        return pltpu.make_async_remote_copy(
            src_ref=buf.at[axis, pos[axis]], dst_ref=buf.at[axis, target],
            send_sem=red_send.at[which, axis, off], recv_sem=red_recv.at[which, axis, off],
            device_id=peer(axis, lax.rem(pos[axis] + off, n)), device_id_type=MESH)

    def red_start(buf, which, axis, tile):
        buf[axis, pos[axis]] = tile
        for off in range(1, sizes[axis]):
            red_copy(buf, which, axis, off, pos[axis]).start()

    def red_finish(buf, which, axis):
        n = sizes[axis]
        for off in range(1, n):
            red_copy(buf, which, axis, off, lax.rem(pos[axis] - off + n, n)).wait_recv()
        total = buf[axis, 0]
        for i in range(1, n):
            total = total + buf[axis, i]
        return total

    rows_a = []
    for h in range(H):
        for d in range(6):
            receive(L0 if h == 0 else L1, d)
            if h == 0:
                receive(PM, d)
            for k in range(2):
                s = 2 * d + k
                if h == 0:
                    hi, lo = split(send_p[s] + recv_p[s])
                    mhl[s, :, :B] = hi
                    mhl[s, :, B:] = lo
                x = send_l[h, s] + recv_l[h, s]
                r[h, s] = x
                z = apply_m(s, x)
                z1[h, s] = z
                zb[h, s * B:(s + 1) * B, :] = z.astype(jnp.bfloat16)
        for d in range(6):
            product(h, d, z1, u1)
            send(U10 + h, d)
        g00 = jnp.zeros((8, W), jnp.float32)
        g01 = jnp.zeros((8, W), jnp.float32)
        for s in range(NS):
            g00 = g00 + fold(r[h, s] * r[h, s])
            g01 = g01 + fold(u1[h, s] * r[h, s])
        rows_a += [0.5 * colsum(g00), colsum(g01)]
    red_start(red_a, 0, 0, jnp.concatenate(rows_a + [jnp.zeros((4, W), jnp.float32)], axis=0))

    for h in range(H):
        for d in range(6):
            receive(U10 + h, d)
            for k in range(2):
                s = 2 * d + k
                x = u1[h, s] + ru1[h, s]
                w1[h, s] = x
                z = apply_m(s, x)
                z2[h, s] = z
                zb[h, s * B:(s + 1) * B, :] = z.astype(jnp.bfloat16)
        for d in range(6):
            product(h, d, z2, u2)
            send(U20 + h, d)
        red_start(red_a, 0, 1 + h, red_finish(red_a, 0, h))
    tot_a = red_finish(red_a, 0, 2)

    rows_b = []
    h11s = []
    for h in range(H):
        h11 = tot_a[2 * h + 1:2 * h + 2] / (tot_a[2 * h:2 * h + 1] + EPS)
        h11s.append(h11)
        gqq = jnp.zeros((8, W), jnp.float32)
        gwr = jnp.zeros((8, W), jnp.float32)
        gwq = jnp.zeros((8, W), jnp.float32)
        for s in range(NS):
            q = w1[h, s] - h11 * r[h, s]
            wq = u2[h, s] - h11 * u1[h, s]
            gqq = gqq + fold(q * q)
            gwr = gwr + fold(wq * r[h, s])
            gwq = gwq + fold(wq * q)
        rows_b.append([0.5 * colsum(gqq), colsum(gwr), colsum(gwq)])
    for h in range(H):
        gww = jnp.zeros((8, W), jnp.float32)
        for d in range(6):
            receive(U20 + h, d)
            s = 2 * d + 1 - d % 2
            v = u2[h, s] + ru2[h, d] - h11s[h] * w1[h, s]
            gww = gww + fold(v * v)
        rows_b[h].append(colsum(gww))
    tile = jnp.concatenate(rows_b[0] + rows_b[1], axis=0)
    for axis in range(3):
        red_start(red_b, 1, axis, tile)
        tile = red_finish(red_b, 1, axis)
    tot_b = tile

    c1s, c2s = [], []
    for h in range(H):
        g00, g01 = [tot_a[2 * h + i:2 * h + i + 1] for i in range(2)]
        gqq, gwr, gwq, gww = [tot_b[4 * h + i:4 * h + i + 1] for i in range(4)]
        beta2 = g00 + EPS
        beta = jnp.sqrt(beta2)
        n1 = g00 / beta2
        h11 = g01 / beta2
        q2 = gqq / beta2
        h21sq = q2 + EPS
        h21 = jnp.sqrt(h21sq)
        n2 = q2 / h21sq
        a = 1.0 / (beta * h21)
        h12 = gwr * a / beta
        h22 = gwq * a * a - h12 * (h11 * (1.0 - n1) / h21)
        ww = gww * a * a
        h32 = jnp.sqrt(jnp.maximum(
            ww - h12 * h12 * (2.0 - n1) - h22 * h22 * (2.0 - n2), 0.0) + EPS)
        r1 = jnp.sqrt(h11 * h11 + h21 * h21)
        cs1 = h11 / r1
        sn1 = h21 / r1
        top = cs1 * h12 + sn1 * h22
        low = cs1 * h22 - sn1 * h12
        r2 = jnp.sqrt(low * low + h32 * h32)
        cs2 = low / r2
        sn2 = h32 / r2
        y2 = -beta * sn1 * cs2 / r2
        y1 = (beta * cs1 - top * y2) / r1
        norm[:, h * W:(h + 1) * W] = beta * sn1 * sn2
        c2 = y2 * a
        c1s.append(y1 / beta - c2 * h11)
        c2s.append(c2)
    for b in range(NB):
        index = jnp.int32(0)
        mask = jnp.float32(0.0)
        for s in range(NS):
            hit = face[0, 0, 0, s // 2, s % 2] == b
            index = jnp.where(hit, s, index)
            mask = jnp.where(hit, 1.0, mask)
        for h in range(H):
            out[b * B:(b + 1) * B, h * W:(h + 1) * W] = mask * (
                c1s[h] * z1[h, index] + c2s[h] * z2[h, index])

    for m in range(7):
        for d in range(6):
            @pl.when(exists(d))
            def _():
                message(m, d).wait_send()
    for which, buf in ((0, red_a), (1, red_b)):
        for axis in range(3):
            for off in range(1, sizes[axis]):
                red_copy(buf, which, axis, off, pos[axis]).wait_send()


def solution(mesh):
    sizes = tuple(mesh.shape[a] for a in AXES)
    f32, bf16 = jnp.float32, jnp.bfloat16
    vmem = pl.BlockSpec(memory_space=pltpu.VMEM)
    smem = pl.BlockSpec(memory_space=pltpu.SMEM)
    hbm = pl.BlockSpec(memory_space=pltpu.HBM)
    blocks = (H, NS, B, W)

    def on_device(schur, interface_diag, precond, load, face_blocks):
        out, norm = pl.pallas_call(
            lambda *refs: main_kernel(sizes, *refs),
            out_shape=(jax.ShapeDtypeStruct((N, H * W), f32), jax.ShapeDtypeStruct((1, H * W), f32)),
            in_specs=[smem, hbm, hbm, hbm, hbm],
            out_specs=(vmem, vmem),
            scratch_shapes=[
                pltpu.VMEM(blocks, f32),
                pltpu.VMEM(blocks, f32),
                pltpu.VMEM((NB, NB, B, B), bf16),
                pltpu.VMEM((NB, B, H * W), bf16),
                pltpu.VMEM((NB, B, B), f32),
                pltpu.VMEM((NB, 1, B), f32),
                pltpu.VMEM((C, C), bf16),
                pltpu.VMEM((NS, B, W), f32),
                pltpu.VMEM(blocks, f32),
                pltpu.VMEM(blocks, f32),
                pltpu.VMEM(blocks, f32),
                pltpu.VMEM((NS, B, B), f32),
                pltpu.VMEM((NS, B, B), f32),
                pltpu.VMEM((NS, B, 2 * B), bf16),
                pltpu.VMEM((H, C, W), bf16),
                pltpu.VMEM(blocks, f32),
                pltpu.VMEM(blocks, f32),
                pltpu.VMEM(blocks, f32),
                pltpu.VMEM(blocks, f32),
                pltpu.VMEM((H, 6, B, W), f32),
                pltpu.VMEM((3, 8, 8, W), f32),
                pltpu.VMEM((3, 8, 8, W), f32),
                pltpu.SemaphoreType.DMA((3 + NB,)),
                pltpu.SemaphoreType.DMA((7, 6)),
                pltpu.SemaphoreType.DMA((7, 6)),
                pltpu.SemaphoreType.DMA((2, 3, 8)),
                pltpu.SemaphoreType.DMA((2, 3, 8)),
            ],
            compiler_params=pltpu.CompilerParams(
                collective_id=0, has_side_effects=True, vmem_limit_bytes=46 * 1024 * 1024),
            name="gmres_steps",
        )(face_blocks, schur.reshape(NB, B, N), interface_diag.reshape(NB, 1, B),
          precond.reshape(NB, B, B), load.reshape(NB, B, H * W))
        return out.reshape(1, 1, 1, N, H * W), norm.reshape(H * W)

    in_specs = (
        P("gx", "gy", "gz", None, None),
        P("gx", "gy", "gz", None),
        P("gx", "gy", "gz", None, None, None),
        P("gx", "gy", "gz", None, None),
        P("gx", "gy", "gz", None, None),
    )
    out_specs = (P("gx", "gy", "gz", None, None), P(None))
    return jax.shard_map(on_device, mesh=mesh, in_specs=in_specs, out_specs=out_specs,
                         check_vma=False)
```

time: 273 us -> 59.6 us (0.22)
  blocking collectives: 82.6 us -> 0 us
  starting transfers between devices: 68.3 us -> 0 us
  local copies, waits for them, and re-layouts: 61.4 us -> 5.79 us
  Pallas kernels: 0 us -> 52.9 us
  other arithmetic: 28.9 us -> 0 us
  matrix products: 23.4 us -> 0 us
  waiting for transfers between devices: 5.76 us -> 0 us
    psum x8 -> x0, blocking collectives: 82.6 us -> none  [one_axis_at_a_time(): return functools.reduce(lax.psum, axes, value)]
    ppermute x24 -> x0, starting transfers between devices: 68.3 us -> none  [the longest x12 50.3 us: extended_2(): before = lax.ppermute(last, axis, up)]
    pallas_call x0 -> x1, Pallas kernels: none -> 52.9 us  [on_device(): pl.pallas_call(lambda *refs: main_kernel(sizes, *refs), out_shape=(jax.Sh...]
    dot_general x4 -> x0, matrix products: 23.4 us -> none  [the longest x2 15.4 us: operate(): product = jnp.dot(matrix, narrow, preferred_element_type=jnp.float32)]
    scatter-add x4 -> x0, other arithmetic: 16.5 us -> none  [assemble(): extended.at[slot_flat]]
    unnamed x39 -> x9, local copies, waits for them, and re-layouts: 17.2 us -> 5.79 us
    gather x4 -> x0, local copies, waits for them, and re-layouts: 10.5 us -> none  [assemble(): packed = extended[slot_flat].reshape(6, slot_count, block_rows, row_width)]
    slice x5 -> x0, local copies, waits for them, and re-layouts: 10.2 us -> none  [the longest x4 7.12 us: assemble(): gz_faces = extended_2(jnp.stack([packed[5], packed[4]], 0), ((GZ, 0),), 1)]
  transfers between devices with their start and end apart: 24 -> 0, of which waited for: 3 -> 0; matrix products, arithmetic and copies ran while one was open for 10% -> 0% of each run, Pallas kernels for 0% -> 0%
where the time goes in v1:
time: 59.6 us; the launch traced here: 59.4 us
  Pallas kernels  52.9 us (89%)
  local copies, waits for them, and re-layouts  5.79 us (10%)
  between operations  0.64 us (1%)
    pallas_call x1, Pallas kernels, on_device(): pl.pallas_call(lambda *refs: main_kernel(sizes, *refs), out_shape=(jax.Sh...  52.9 us
    unnamed x9, local copies, waits for them, and re-layouts  5.79 us

profile of v1, /device:TPU:1, one launch (start us, length us, event | category | flops | bytes accessed | tf_op | source)
XLA Modules:
  0.0 59.4 jit_solution(15466462759479813174)
XLA Ops:
  0.6 0.8 %copy.7.refs_0_ = s32[1,1,1,6,2]{4,3,2,1,0:T(8,128)S(1)} copy(s32[1,1,1,6,2]{3,4,2,1,0:T(2,128)} %param.9) | data formatting | bytes 96 | tf_op args[4]
  1.4 0.0 copy-start
  1.4 1.2 %copy-done = f32[1,1,1,16,128,128]{5,4,3,2,1,0:T(8,128)S(1)} copy-done((f32[1,1,1,16,128,128]{5,4,3,2,1,0:T(8,128)S(1)}, f32[1,1,1,16,128,128]{5,4,3,2,1,0:T(8,128)}, u32[]{:S(2)}) %copy-start) | copy-done | bytes 1048600
  2.6 0.0 copy-start.1
  2.6 1.2 %copy-done.1 = bf16[1,1,1,2048,256]{4,3,2,1,0:T(8,128)(2,1)S(1)} copy-done((bf16[1,1,1,2048,256]{4,3,2,1,0:T(8,128)(2,1)S(1)}, bf16[1,1,1,2048,256]{4,3,2,1,0:T(8,128)(2,1)}, u32[]{:S(2)}) %copy-start.1) | copy-done | bytes 1048600
  3.8 0.0 copy-start.2
  3.8 0.7 %copy-done.2 = f32[1,1,1,2048]{3,2,1,0:T(1,128)S(1)} copy-done((f32[1,1,1,2048]{3,2,1,0:T(1,128)S(1)}, f32[1,1,1,2048]{3,2,1,0:T(1,128)}, u32[]{:S(2)}) %copy-start.2) | copy-done | bytes 8216
  4.5 52.9 %gmres_steps.1 = (f32[2048,256]{1,0:T(8,128)S(1)}, f32[1,256]{1,0:T(1,128)S(1)}) custom-call(s32[1,1,1,6,2]{4,3,2,1,0:T(8,128)S(1)} %copy.7.refs_0_, bf16[16,128,2048]{2,1,0:T(8,128)(2,1)} %bitcast.11, f32[16,1,128]{2,1,0:T(1,128)S(1)} %bitcast.9, f32[16,128,128]{2,1,0:T(8,128)S(1)} %bitcast.7, bf16[16,128,256]{2,1,0:T(8,128)(2,1)S(1)} %bitcast.8), custom_call_target="tpu_custom_call" | custom-call | tf_op jit(solution)/shard_map/gmres_steps/pallas_call | solution.py:348
  57.5 1.3 %copy.10 = f32[1,1,1,2048,256]{4,3,2,1,0:T(8,128)} copy(f32[1,1,1,2048,256]{4,3,2,1,0:T(8,128)S(1)} %bitcast.6) | data formatting | bytes 4194304
  58.8 0.6 copy.11
Async XLA Ops:
  1.4 1.2 %copy-start = (f32[1,1,1,16,128,128]{5,4,3,2,1,0:T(8,128)S(1)}, f32[1,1,1,16,128,128]{5,4,3,2,1,0:T(8,128)}, u32[]{:S(2)}) copy-start(f32[1,1,1,16,128,128]{5,4,3,2,1,0:T(8,128)} %param.7) | copy-start | bytes 3145732
  2.6 1.2 %copy-start.1 = (bf16[1,1,1,2048,256]{4,3,2,1,0:T(8,128)(2,1)S(1)}, bf16[1,1,1,2048,256]{4,3,2,1,0:T(8,128)(2,1)}, u32[]{:S(2)}) copy-start(bf16[1,1,1,2048,256]{4,3,2,1,0:T(8,128)(2,1)} %param.8) | copy-start | bytes 3145732
  3.8 0.7 %copy-start.2 = (f32[1,1,1,2048]{3,2,1,0:T(1,128)S(1)}, f32[1,1,1,2048]{3,2,1,0:T(1,128)}, u32[]{:S(2)}) copy-start(f32[1,1,1,2048]{3,2,1,0:T(1,128)} %param.6) | copy-start | bytes 24580
